TPU v7x, 32 devices: a whole 2x2x4 slice. The times are simulated.
32 devices in a mesh: inter: 16 (over z, y, core), intra: 2 (over x).
Axes of the slice: x: 2, y: 2, z: 4, core: 2. Of those that a mesh axis runs over, the one named last changes fastest.
Arguments:
- partials: bfloat16 [32, 16, 5120], P(('inter', 'intra')), may hold values from -6 to 6
- scales: bfloat16 [32, 16, 20], P(('inter', 'intra')), may hold values from 64 to 1024
- overflow_pos: int32 [32, 1], P(('inter', 'intra')), may hold values from -81920 to 81919, as said below
- weights: float32 [16, 5120], P('inter', 'intra'), may hold values from -6 to 6
- exponent: int32 [], replicated, may hold values from 10 to 16
Outputs:
- grad_out: float32 [16, 5120], P('inter', 'intra')
- block_scale: float32 [16, 20], P('inter', 'intra')
- master_out: float32 [16, 5120], P('inter', 'intra')
- new_exponent: int32 [], replicated
- overflow_count: int32 [], replicated
Inputs may be any that keep to these rules, and one draw needn't show every extreme that they name: `overflow_pos`: A negative entry means no overflow on that device; otherwise it is the flat position (row times 5120 plus column) of an overflowed value of that device's partial.
All inputs are finite; a program needn't handle non-finite values.
Results may differ from a plain program's by a relative error of at most 0.0005.
Values may be sent and summed in bfloat16 or wider, within the bound.
A program may use at most 64 MiB of HBM per device.

v0:
```python
import jax
import jax.numpy as jnp
from jax import lax
from jax.sharding import PartitionSpec as P


def dequantize(levels, block_scales, block_len):
    dims_all = levels.shape
    expanded = levels.astype(jnp.float32).reshape(
        dims_all[0], dims_all[1], dims_all[2], block_scales.shape[3], block_len
    )
    expanded = expanded * block_scales.astype(jnp.float32)[..., None]
    return jnp.sum(expanded, axis=2).reshape(dims_all[0], dims_all[1], dims_all[3])


def on_device(partials, scales, overflow_pos, weights, exponent):
    inter_size = lax.axis_size("inter")
    intra_size = lax.axis_size("intra")
    row_total = partials.shape[1]
    full_width = partials.shape[2]
    block_total = scales.shape[2]
    block_len = full_width // block_total
    share_rows = row_total // inter_size
    share_cols = full_width // intra_size
    share_blocks = block_total // intra_size
    local_flags = jnp.sum((overflow_pos >= 0).astype(jnp.float32))
    grouped = partials.reshape(inter_size, share_rows, intra_size, share_cols)
    grouped_scales = scales.reshape(inter_size, share_rows, intra_size, share_blocks)
    flag_copies = jnp.full((1, 1, intra_size, 1), local_flags, jnp.bfloat16)
    got_levels, got_scales, got_flags = (
        lax.all_to_all(grouped, "intra", split_axis=2, concat_axis=2, tiled=True),
        lax.all_to_all(grouped_scales, "intra", split_axis=2, concat_axis=2, tiled=True),
        lax.all_to_all(flag_copies, "intra", split_axis=2, concat_axis=2, tiled=True),
    )
    group_sum = dequantize(got_levels, got_scales, block_len)
    group_flags = jnp.sum(got_flags.astype(jnp.float32))
    grad_sum = lax.psum_scatter(group_sum, "inter", scatter_dimension=0, tiled=True)[0]
    flag_total = lax.psum(group_flags, "inter")
    flag_count = flag_total.astype(jnp.int32)
    grad_out = grad_sum * jnp.exp2(-exponent.astype(jnp.float32))
    block_scale = (
        jnp.max(jnp.abs(grad_out.reshape(share_rows, share_blocks, block_len)), axis=2) / 127.0
    )
    master_out = jnp.where(flag_count == 0, weights - 0.5 * grad_out, weights)
    new_exponent = exponent - (flag_count > 0).astype(jnp.int32)
    return (grad_out, block_scale, master_out, new_exponent, flag_count)


def solution(mesh):
    placed = (
        P(("inter", "intra"), None, None),
        P(("inter", "intra"), None, None),
        P(("inter", "intra"), None),
        P("inter", "intra"),
        P(),
    )
    return jax.shard_map(
        on_device,
        mesh=mesh,
        in_specs=placed,
        out_specs=(P("inter", "intra"), P("inter", "intra"), P("inter", "intra"), P(), P()),
        check_vma=False,
    )
```

profile of v0, /device:TPU:0, one launch (start us, length us, event | category | flops | bytes accessed | tf_op | source)
XLA Modules:
  0.0 137.4 jit_solution(6405079507612451048)
XLA Ops:
  7.2 0.8 reshape.91
  7.9 0.6 copy.15
  8.5 4.2 %all-to-all-start.1 = ((bf16[16,1,2,10]{3,0,1,2:T(8,128)(2,1)}), bf16[16,1,2,10]{3,0,1,2:T(8,128)(2,1)S(1)}, u32[]{:S(2)}, u32[]{:S(2)}) async-start(bf16[16,1,2,10]{3,0,1,2:T(8,128)(2,1)} %copy.15), calls=%async_computation.1 | async-start | bytes 16384 | tf_op jit(solution)/shard_map/all_to_all | solution.py:32
  14.1 1.0 reshape.90
  15.2 0.7 copy.13
  15.8 0.8 all-to-all-done.1
  16.6 3.4 %all-to-all-start = ((bf16[16,1,2,2560]{3,0,1,2:T(8,128)(2,1)}), bf16[16,1,2,2560]{3,0,1,2:T(8,128)(2,1)S(1)}, u32[]{:S(2)}, u32[]{:S(2)}) async-start(bf16[16,1,2,2560]{3,0,1,2:T(8,128)(2,1)} %copy.13), calls=%async_computation | async-start | bytes 327680 | tf_op jit(solution)/shard_map/all_to_all | solution.py:31
  20.0 0.1 mul.67
  20.2 0.1 mul.68
  20.2 4.4 %all-to-all-done = bf16[16,1,2,2560]{3,0,1,2:T(8,128)(2,1)S(1)} async-done(((bf16[16,1,2,2560]{3,0,1,2:T(8,128)(2,1)}), bf16[16,1,2,2560]{3,0,1,2:T(8,128)(2,1)S(1)}, u32[]{:S(2)}, u32[]{:S(2)}) %all-to-all-start) | async-done | bytes 163872 | tf_op jit(solution)/shard_map/all_to_all | solution.py:31
  24.7 0.6 broadcast_in_dim.4
  25.2 3.2 %all-to-all-start.2 = ((bf16[1,1,2,1]{3,1,0,2:T(2,128)(2,1)}), bf16[1,1,2,1]{3,1,0,2:T(2,128)(2,1)S(1)}, u32[]{:S(2)}, u32[]{:S(2)}) async-start(bf16[1,1,2,1]{3,1,0,2:T(2,128)(2,1)} %broadcast_in_dim.4), calls=%async_computation.2 | async-start | bytes 2048 | tf_op jit(solution)/shard_map/all_to_all | solution.py:33
  28.4 0.0 all-reduce.3.cloned.1.call-start
  28.5 0.7 multiply_reduce_fusion
  29.2 2.9 %all-to-all-done.2 = bf16[1,1,2,1]{3,1,0,2:T(2,128)(2,1)S(1)} async-done(((bf16[1,1,2,1]{3,1,0,2:T(2,128)(2,1)}), bf16[1,1,2,1]{3,1,0,2:T(2,128)(2,1)S(1)}, u32[]{:S(2)}, u32[]{:S(2)}) %all-to-all-start.2) | async-done | bytes 36 | tf_op jit(solution)/shard_map/all_to_all | solution.py:33
  32.1 0.6 convert_reduce_fusion
  32.7 0.7 dynamic-slice
  33.4 31.5 %psum.7 = f32[]{:T(128)} all-reduce(f32[]{:T(128)} %convert_reduce_fusion), channel_id=1, replica_groups=mesh['inter'=16,'intra'=2] {'inter'}, use_global_device_ids=true, to_apply=%region_4.0 | all-reduce | flops 1 | bytes 8 | tf_op jit(solution)/shard_map/psum | solution.py:38
  65.6 58.2 %all-reduce.3.cloned.1.call-done = f32[16,1,2560]{2,0,1:T(8,128)} async-done(((f32[16,1,2560]{2,0,1:T(8,128)}), f32[16,1,2560]{2,0,1:T(8,128)}) %all-reduce.3.cloned.1.call-update) | async-done | bytes 163856
  123.8 1.6 %abs_reduce_fusion = f32[2560]{0:T(1024)S(1)} fusion(f32[]{:T(128)S(6)} %exp2.7, f32[16,1,2560]{2,0,1:T(8,128)} %all-reduce.3.cloned.1.call-done, u32[]{:T(128)} %bitcast.3), kind=kLoop, calls=%fused_computation.3 | loop fusion | flops 5120 | bytes 20488 | tf_op jit(solution)/shard_map/abs | solution.py:42
  125.4 0.1 reduce_max.9
  125.5 0.5 multiply_bitcast_fusion
  126.0 0.1 copy-done
  126.1 2.2 %broadcast_select_fusion = (f32[1,2560]{1,0:T(1,128)}, f32[1,2560]{1,0:T(1,128)}) fusion(f32[1,2560]{1,0:T(1,128)S(1)} %copy-done, pred[]{:T(512)S(6)} %eq.3, f32[]{:T(128)S(6)} %exp2.7, f32[16,1,2560]{2,0,1:T(8,128)} %all-reduce.3.cloned.1.call-done, u32[]{:T(128)} %bitcast.3), kind=kLoop, calls=%fused_computation.1 | loop fusion | flops 10240 | bytes 40969 | tf_op jit(solution)/shard_map/jit(_where)/select_n | solution.py:44
  (6 shorter events, 0.0 us)
Async XLA Ops:
  8.5 8.1 %all-to-all-start.1 = ((bf16[16,1,2,10]{3,0,1,2:T(8,128)(2,1)}), bf16[16,1,2,10]{3,0,1,2:T(8,128)(2,1)S(1)}, u32[]{:S(2)}, u32[]{:S(2)}) async-start(bf16[16,1,2,10]{3,0,1,2:T(8,128)(2,1)} %copy.15), calls=%async_computation.1 | async-start | bytes 16384 | tf_op jit(solution)/shard_map/all_to_all | solution.py:32
  16.6 8.1 %all-to-all-start = ((bf16[16,1,2,2560]{3,0,1,2:T(8,128)(2,1)}), bf16[16,1,2,2560]{3,0,1,2:T(8,128)(2,1)S(1)}, u32[]{:S(2)}, u32[]{:S(2)}) async-start(bf16[16,1,2,2560]{3,0,1,2:T(8,128)(2,1)} %copy.13), calls=%async_computation | async-start | bytes 327680 | tf_op jit(solution)/shard_map/all_to_all | solution.py:31
  25.2 6.9 %all-to-all-start.2 = ((bf16[1,1,2,1]{3,1,0,2:T(2,128)(2,1)}), bf16[1,1,2,1]{3,1,0,2:T(2,128)(2,1)S(1)}, u32[]{:S(2)}, u32[]{:S(2)}) async-start(bf16[1,1,2,1]{3,1,0,2:T(2,128)(2,1)} %broadcast_in_dim.4), calls=%async_computation.2 | async-start | bytes 2048 | tf_op jit(solution)/shard_map/all_to_all | solution.py:33
  28.4 95.4 %all-reduce.3.cloned.1.call-start = ((), (), s32[]{:S(2)}) async-start(), calls=%async_computation.3 | async-start | bytes 327680
  29.2 3.5 %copy-start.1 = (u32[32]{0:T(128)S(1)}, u32[32]{0:T(128)}, u32[]{:S(2)}) copy-start(u32[32]{0:T(128)} %constant.21) | copy-start | bytes 388
  125.4 0.7 copy-start
Sparse Core Ops, SparseCore 0:
  32.7 91.0 all-reduce.2
where the time goes:
time: 138 us; the launch traced here: 137 us
  waiting for transfers between devices  66.3 us (48%)
  blocking collectives  31.5 us (23%)
  between operations  18.4 us (13%)
  starting transfers between devices  10.9 us (8%)
  other arithmetic  5.74 us (4%)
  local copies, waits for them, and re-layouts  4.56 us (3%)
    unnamed x2, waiting for transfers between devices  58.2 us
    psum x1, blocking collectives, on_device(): flag_total = lax.psum(group_flags, 'inter')  31.5 us
    all_to_all x1, waiting for transfers between devices, on_device(): lax.all_to_all(grouped, 'intra', split_axis=2, concat_axis=2, tiled=True)  4.42 us
    all_to_all x1, starting transfers between devices, on_device(): lax.all_to_all(grouped_scales, 'intra', split_axis=2, concat_axis=2, tile...  4.23 us
    all_to_all x1, starting transfers between devices, on_device(): lax.all_to_all(grouped, 'intra', split_axis=2, concat_axis=2, tiled=True)  3.43 us
    all_to_all x1, starting transfers between devices, on_device(): lax.all_to_all(flag_copies, 'intra', split_axis=2, concat_axis=2, tiled=T...  3.19 us
    all_to_all x1, waiting for transfers between devices, on_device(): lax.all_to_all(flag_copies, 'intra', split_axis=2, concat_axis=2, tiled=T...  2.91 us
  transfers between devices with their start and end apart: 4, of which 4 were waited for; matrix products, arithmetic and copies ran while one was open for 3% of the time, Pallas kernels for 0%

commit v1 on v0

v1 whole, which is shorter than its diff:
```python
import functools

import jax
import jax.numpy as jnp
from jax import lax
from jax.experimental import pallas as pl
from jax.experimental.pallas import tpu as pltpu
from jax.sharding import PartitionSpec as P

LANES = 128
ROW_GROUP = 16
SOURCE_GROUP = 32


def exchange(inter_size, intra_size, block_len, x_hbm, s_hbm, pos_ref, out_ref, xv, sv, staged, outgoing, incoming,
             load_sems, own_sem, send_sem, recv_sem):
    total = inter_size * intra_size
    row_total, full_width = xv.shape
    block_total = sv.shape[1]
    share_cols = full_width // intra_size
    half = share_cols // 2
    tiles = half // LANES
    my_inter = lax.axis_index("inter")
    my_intra = lax.axis_index("intra")
    me = my_inter * intra_size + my_intra

    load_x = pltpu.make_async_copy(x_hbm.at[0], xv, load_sems.at[0])
    load_s = pltpu.make_async_copy(s_hbm.at[0], sv, load_sems.at[1])
    load_x.start()
    load_s.start()

    barrier = pltpu.get_barrier_semaphore()

    def peer(k):
        target = lax.rem(me + k, total)
        return target // intra_size, lax.rem(target, intra_size)

    def greet(k, carry):
        pl.semaphore_signal(barrier, inc=1, device_id=peer(k), device_id_type=pl.DeviceIdType.MESH)
        return carry

    lax.fori_loop(1, total, greet, 0)

    load_x.wait()
    load_s.wait()
    flag = jnp.where(pos_ref[0, 0] >= 0, jnp.float32(1), jnp.float32(0))
    lane = lax.broadcasted_iota(jnp.int32, (ROW_GROUP, LANES), 1)
    pick_block = lax.broadcasted_iota(jnp.int32, (block_total, LANES), 0)
    pick_lane = lax.broadcasted_iota(jnp.int32, (block_total, LANES), 1)

    def stage(group, carry):
        first = pl.multiple_of(group * ROW_GROUP, ROW_GROUP)
        rows = pl.ds(first, ROW_GROUP)
        scale_rows = sv[rows, :]
        for b in range(intra_size):
            for h in range(2):
                start = (b * 2 + h) * half
                staged[:, b, h, pl.ds(0, half)] = xv[rows, pl.ds(start, half)].astype(jnp.float32)
                hit = (pick_block == (start + pick_lane * LANES) // block_len) & (pick_lane < tiles)
                spread = jnp.dot(scale_rows, hit.astype(jnp.float32).astype(jnp.bfloat16),
                                 preferred_element_type=jnp.float32)
                staged[:, b, h, pl.ds(half, LANES)] = jnp.where(lane == tiles, flag, spread)
        outgoing[rows] = staged[...].astype(jnp.bfloat16)
        return carry

    lax.fori_loop(0, row_total // ROW_GROUP, stage, 0)

    own = pltpu.make_async_copy(outgoing.at[my_inter, my_intra], incoming.at[me], own_sem)
    own.start()
    pl.semaphore_wait(barrier, total - 1)

    def send(k, carry):
        to_inter, to_intra = peer(k)
        pltpu.make_async_remote_copy(
            src_ref=outgoing.at[to_inter, to_intra],
            dst_ref=incoming.at[me],
            send_sem=send_sem,
            recv_sem=recv_sem,
            device_id=(to_inter, to_intra),
            device_id_type=pl.DeviceIdType.MESH,
        ).start()
        return carry

    lax.fori_loop(1, total, send, 0)
    own.wait()
    others = incoming.at[pl.ds(0, total - 1)]
    pltpu.make_async_copy(others, others, recv_sem).wait()

    def reduce(group, sums):
        sources = pl.ds(group * SOURCE_GROUP, SOURCE_GROUP)
        factors = incoming[sources, :, pl.ds(half, LANES)].astype(jnp.float32)
        added = [
            jnp.sum(incoming[sources, :, pl.ds(t * LANES, LANES)].astype(jnp.float32) * factors[:, :, t:t + 1], axis=0)
            for t in range(tiles)
        ]
        added.append(jnp.sum(factors, axis=0))
        return tuple(s + a for s, a in zip(sums, added))

    sums = tuple(jnp.zeros((2, LANES), jnp.float32) for _ in range(tiles + 1))
    sums = lax.fori_loop(0, total // SOURCE_GROUP, reduce, sums)
    for t in range(tiles):
        for h in range(2):
            out_ref[0:1, pl.ds(h * half + t * LANES, LANES)] = sums[t][h:h + 1]
    out_ref[0:1, pl.ds(share_cols, LANES)] = sums[tiles][0:1]
    pltpu.make_async_copy(others, others, send_sem).wait()


def finish(block_len, sum_ref, w_ref, e_ref, grad_ref, scale_ref, master_ref, exp_ref, count_ref):
    share_cols = w_ref.shape[1]
    blocks = share_cols // block_len
    tiles = share_cols // 2 // LANES
    counts = sum_ref[0:1, pl.ds(share_cols, LANES)]
    lane = lax.broadcasted_iota(jnp.int32, (1, LANES), 1)
    count = jnp.sum(jnp.where(lane == tiles, counts, 0.0)).astype(jnp.int32)
    exponent = e_ref[0, 0]
    unscale = jnp.exp2(jnp.full((1, LANES), -exponent.astype(jnp.float32), jnp.float32))[:, 0:1]
    grad = sum_ref[0:1, pl.ds(0, share_cols)] * unscale
    grad_ref[...] = grad
    weights = w_ref[...]
    master_ref[...] = jnp.where(count == 0, weights - 0.5 * grad, weights)
    block_lane = lax.broadcasted_iota(jnp.int32, (1, blocks), 1)
    largest = jnp.zeros((1, blocks), jnp.float32)
    for n in range(blocks):
        top = jnp.max(jnp.abs(grad[:, n * block_len:(n + 1) * block_len]), axis=1, keepdims=True)
        largest = jnp.where(block_lane == n, top, largest)
    scale_ref[...] = largest / 127.0
    exp_ref[0] = exponent - jnp.where(count > 0, 1, 0)
    count_ref[0] = count


def on_device(partials, scales, overflow_pos, weights, exponent):
    inter_size = lax.axis_size("inter")
    intra_size = lax.axis_size("intra")
    total = inter_size * intra_size
    row_total, full_width = partials.shape[1], partials.shape[2]
    block_total = scales.shape[2]
    block_len = full_width // block_total
    share_cols = full_width // intra_size
    width = share_cols // 2 + LANES
    any_space = pl.BlockSpec(memory_space=pl.ANY)
    vmem = pl.BlockSpec(memory_space=pltpu.VMEM)
    smem = pl.BlockSpec(memory_space=pltpu.SMEM)
    sums = pl.pallas_call(
        functools.partial(exchange, inter_size, intra_size, block_len),
        out_shape=jax.ShapeDtypeStruct((1, share_cols + LANES), jnp.float32),
        in_specs=[any_space, any_space, smem],
        out_specs=vmem,
        scratch_shapes=[
            pltpu.VMEM((row_total, full_width), jnp.bfloat16),
            pltpu.VMEM((row_total, block_total), jnp.bfloat16),
            pltpu.VMEM((ROW_GROUP, intra_size, 2, width), jnp.float32),
            pltpu.VMEM((row_total, intra_size, 2, width), jnp.bfloat16),
            pltpu.VMEM((total, 2, width), jnp.bfloat16),
            pltpu.SemaphoreType.DMA((2,)),
            pltpu.SemaphoreType.DMA,
            pltpu.SemaphoreType.DMA,
            pltpu.SemaphoreType.DMA,
        ],
        compiler_params=pltpu.CompilerParams(collective_id=0, has_side_effects=True),
        name="exchange",
    )(partials, scales, overflow_pos)
    grad_out, block_scale, master_out, new_exponent, count = pl.pallas_call(
        functools.partial(finish, block_len),
        out_shape=(
            jax.ShapeDtypeStruct((1, share_cols), jnp.float32),
            jax.ShapeDtypeStruct((1, share_cols // block_len), jnp.float32),
            jax.ShapeDtypeStruct((1, share_cols), jnp.float32),
            jax.ShapeDtypeStruct((1,), jnp.int32),
            jax.ShapeDtypeStruct((1,), jnp.int32),
        ),
        in_specs=[vmem, vmem, smem],
        out_specs=(vmem, vmem, vmem, smem, smem),
        name="finish",
    )(sums, weights, exponent.reshape(1, 1))
    return grad_out, block_scale, master_out, new_exponent.reshape(()), count.reshape(())


def solution(mesh):
    placed = (
        P(("inter", "intra"), None, None),
        P(("inter", "intra"), None, None),
        P(("inter", "intra"), None),
        P("inter", "intra"),
        P(),
    )
    return jax.shard_map(
        on_device,
        mesh=mesh,
        in_specs=placed,
        out_specs=(P("inter", "intra"), P("inter", "intra"), P("inter", "intra"), P(), P()),
        check_vma=False,
    )
```

time: 138 us -> 15.5 us (0.11)
  waiting for transfers between devices: 66.3 us -> 0 us
  blocking collectives: 31.5 us -> 0 us
  between operations: 18.4 us -> 1.93 us
  Pallas kernels: 0 us -> 13.4 us
  starting transfers between devices: 10.9 us -> 0 us
  other arithmetic: 5.74 us -> 0 us
  local copies, waits for them, and re-layouts: 4.56 us -> 0 us
    unnamed x2 -> x0, waiting for transfers between devices: 58.2 us -> none
    psum x1 -> x0, blocking collectives: 31.5 us -> none  [on_device(): flag_total = lax.psum(group_flags, 'inter')]
    pallas_call x0 -> x2, Pallas kernels: none -> 13.4 us  [the longest x1 11.9 us: on_device(): pl.pallas_call(functools.partial(exchange, inter_size, intra_size, block_...]
    all_to_all x3 -> x0, starting transfers between devices: 10.9 us -> none  [the longest x1 4.23 us: on_device(): lax.all_to_all(grouped_scales, 'intra', split_axis=2, concat_axis=2, tile...]
    all_to_all x3 -> x0, waiting for transfers between devices: 8.09 us -> none  [the longest x1 4.42 us: on_device(): lax.all_to_all(grouped, 'intra', split_axis=2, concat_axis=2, tiled=True)]
    reshape x4 -> x0, local copies, waits for them, and re-layouts: 3.07 us -> none  [the longest x2 1.7 us: on_device(): grouped = partials.reshape(inter_size, share_rows, intra_size, share_cols)]
    select_n x1 -> x0, other arithmetic: 2.2 us -> none  [on_device(): master_out = jnp.where(flag_count == 0, weights - 0.5 * grad_out, weights)]
    abs x1 -> x0, other arithmetic: 1.62 us -> none  [on_device(): jnp.abs(grad_out.reshape(share_rows, share_blocks, block_len))]
  transfers between devices with their start and end apart: 4 -> 0, of which waited for: 4 -> 0; matrix products, arithmetic and copies ran while one was open for 3% -> 0% of each run, Pallas kernels for 0% -> 0%
where the time goes in v1:
time: 15.5 us; the launch traced here: 15.3 us
  Pallas kernels  13.4 us (86%)
  between operations  1.93 us (12%)
    pallas_call x1, Pallas kernels, on_device(): pl.pallas_call(functools.partial(exchange, inter_size, intra_size, block_...  11.9 us
    pallas_call x1, Pallas kernels, on_device(): pl.pallas_call(functools.partial(finish, block_len), out_shape=(jax.Shape...  1.46 us

profile of v1, /device:TPU:0, one launch (start us, length us, event | category | flops | bytes accessed | tf_op | source)
XLA Modules:
  0.0 15.3 jit_solution(17277857019378999834)
XLA Ops:
  1.9 11.9 %exchange.1.sum_ref = f32[1,2688]{1,0:T(1,128)} custom-call(bf16[1,16,5120]{2,1,0:T(8,128)(2,1)} %x_hbm.1, bf16[1,16,20]{2,1,0:T(8,128)(2,1)} %s_hbm.1, s32[1,1]{1,0:T(1,128)S(6)} %copy.10.pos_ref), custom_call_target="tpu_custom_call" | custom-call | tf_op jit(solution)/shard_map/exchange/pallas_call | solution.py:143
  13.8 1.5 %finish.1 = (f32[1,2560]{1,0:T(1,128)}, f32[1,10]{1,0:T(1,128)}, f32[1,2560]{1,0:T(1,128)}, s32[1]{0:T(128)}, s32[1]{0:T(128)}) custom-call(f32[1,2688]{1,0:T(1,128)} %exchange.1.sum_ref, f32[1,2560]{1,0:T(1,128)} %w_ref.1, s32[1,1]{1,0:T(1,128)} %bitcast.3.e_ref), custom_call_target="tpu_custom_call" | custom-call | tf_op jit(solution)/shard_map/finish/pallas_call | solution.py:162

commit v2 on v1

v2 whole, which is shorter than its diff:
```python
import functools

import jax
import jax.numpy as jnp
from jax import lax
from jax.experimental import pallas as pl
from jax.experimental.pallas import tpu as pltpu
from jax.sharding import PartitionSpec as P

LANES = 128
ROW_GROUP = 16
SOURCE_GROUP = 32


def exchange(inter_size, intra_size, block_len, x_hbm, s_hbm, pos_hbm, w_hbm, e_hbm,
             grad_ref, scale_ref, master_ref, whole_ref,
             xv, sv, pos_ref, w_ref, e_ref, staged, outgoing, incoming,
             load_sems, own_sem, send_sem, recv_sem):
    total = inter_size * intra_size
    row_total, full_width = xv.shape
    block_total = sv.shape[1]
    share_cols = full_width // intra_size
    half = share_cols // 2
    tiles = half // LANES
    my_inter = lax.axis_index("inter")
    my_intra = lax.axis_index("intra")
    me = my_inter * intra_size + my_intra

    loads = [
        pltpu.make_async_copy(src, dst, load_sems.at[n])
        for n, (src, dst) in enumerate(
            ((x_hbm.at[0], xv), (s_hbm.at[0], sv), (pos_hbm, pos_ref), (w_hbm, w_ref), (e_hbm, e_ref))
        )
    ]
    for load in loads:
        load.start()

    barrier = pltpu.get_barrier_semaphore()
    paired = total & (total - 1) == 0 and False
    flips = [bit * (1 - 2 * lax.rem(me // bit, 2)) for bit in (2**n for n in range(total.bit_length() - 1))]

    def peer(k):
        if paired:
            target = me + sum(flip for n, flip in enumerate(flips) if k >> n & 1)
        else:
            target = lax.rem(me + k, total)
        return target // intra_size, lax.rem(target, intra_size)

    def each_peer(visit):
        if paired:
            for k in reversed(range(1, total)):
                visit(k)
        else:
            lax.fori_loop(1, total, lambda k, carry: (visit(k), carry)[1], 0)

    def greet(k):
        pl.semaphore_signal(barrier, inc=1, device_id=peer(k), device_id_type=pl.DeviceIdType.MESH)

    if True:
        each_peer(greet)

    for load in loads[:3]:
        load.wait()
    flag = jnp.where(pos_ref[0, 0] >= 0, jnp.float32(1), jnp.float32(0))
    lane = lax.broadcasted_iota(jnp.int32, (ROW_GROUP, LANES), 1)
    pick_block = lax.broadcasted_iota(jnp.int32, (block_total, LANES), 0)
    pick_lane = lax.broadcasted_iota(jnp.int32, (block_total, LANES), 1)

    def stage(group, carry):
        first = pl.multiple_of(group * ROW_GROUP, ROW_GROUP)
        rows = pl.ds(first, ROW_GROUP)
        scale_rows = sv[rows, :]
        for b in range(intra_size):
            for h in range(2):
                start = (b * 2 + h) * half
                staged[:, b, h, pl.ds(0, half)] = xv[rows, pl.ds(start, half)].astype(jnp.float32)
                hit = (pick_block == (start + pick_lane * LANES) // block_len) & (pick_lane < tiles)
                spread = jnp.dot(scale_rows, hit.astype(jnp.float32).astype(jnp.bfloat16),
                                 preferred_element_type=jnp.float32)
                staged[:, b, h, pl.ds(half, LANES)] = jnp.where(lane == tiles, flag, spread)
        outgoing[rows] = staged[...].astype(jnp.bfloat16)
        return carry

    if True:
        lax.fori_loop(0, row_total // ROW_GROUP, stage, 0)

    own = pltpu.make_async_copy(outgoing.at[my_inter, my_intra], incoming.at[me], own_sem)
    own.start()
    if True:
        pl.semaphore_wait(barrier, total - 1)

    def send(k):
        to_inter, to_intra = peer(k)
        pltpu.make_async_remote_copy(
            src_ref=outgoing.at[to_inter, to_intra],
            dst_ref=incoming.at[me],
            send_sem=send_sem,
            recv_sem=recv_sem,
            device_id=(to_inter, to_intra),
            device_id_type=pl.DeviceIdType.MESH,
        ).start()

    if True:
        each_peer(send)
    for load in loads[3:]:
        load.wait()
    exponent = e_ref[0]
    unscale = jnp.exp2(jnp.full((1, LANES), -exponent.astype(jnp.float32), jnp.float32))
    own.wait()
    others = incoming.at[pl.ds(0, total - 1)]
    if True:
        pltpu.make_async_copy(others, others, recv_sem).wait()

    def reduce(group, sums):
        sources = pl.ds(group * SOURCE_GROUP, SOURCE_GROUP)
        factors = incoming[sources, :, pl.ds(half, LANES)].astype(jnp.float32)
        added = [
            jnp.sum(incoming[sources, :, pl.ds(t * LANES, LANES)].astype(jnp.float32) * factors[:, :, t:t + 1], axis=0)
            for t in range(tiles)
        ]
        added.append(jnp.sum(factors, axis=0))
        return tuple(s + a for s, a in zip(sums, added))

    sums = tuple(jnp.zeros((2, LANES), jnp.float32) for _ in range(tiles + 1))
    if True:
        if total == SOURCE_GROUP:
            sums = reduce(0, sums)
        else:
            sums = lax.fori_loop(0, total // SOURCE_GROUP, reduce, sums)
    lane = lax.broadcasted_iota(jnp.int32, (1, LANES), 1)
    count = jnp.sum(jnp.where(lane == tiles, sums[tiles][0:1], 0.0)).astype(jnp.int32)
    blocks = share_cols // block_len
    per_block = block_len // LANES
    block_lane = lax.broadcasted_iota(jnp.int32, (1, blocks), 1)
    largest = jnp.zeros((1, blocks), jnp.float32)
    tops = []
    for h in range(2):
        for t in range(tiles):
            grad = sums[t][h:h + 1] * unscale
            columns = pl.ds(h * half + t * LANES, LANES)
            grad_ref[0:1, columns] = grad
            weights = w_ref[0:1, columns]
            master_ref[0:1, columns] = jnp.where(count == 0, weights - 0.5 * grad, weights)
            tops.append(jnp.abs(grad))
    for n in range(blocks):
        top = functools.reduce(jnp.maximum, tops[n * per_block:(n + 1) * per_block])
        largest = jnp.where(block_lane == n, jnp.max(top, axis=1, keepdims=True), largest)
    scale_ref[...] = largest / 127.0
    whole_ref[0:1, pl.ds(0, LANES)] = jnp.full((1, LANES), exponent - jnp.where(count > 0, 1, 0), jnp.int32)
    whole_ref[0:1, pl.ds(LANES, LANES)] = jnp.full((1, LANES), count, jnp.int32)
    if True:
        pltpu.make_async_copy(others, others, send_sem).wait()


def finish(grad_in, scale_in, master_in, whole_in, grad_ref, scale_ref, master_ref, exp_ref, count_ref, sems):
    copies = [
        pltpu.make_async_copy(src, dst, sems.at[n])
        for n, (src, dst) in enumerate(((grad_in, grad_ref), (scale_in, scale_ref), (master_in, master_ref)))
    ]
    for copy in copies:
        copy.start()
    exp_ref[0] = whole_in[0:1, 0:1][0, 0]
    count_ref[0] = whole_in[0:1, LANES:LANES + 1][0, 0]
    for copy in copies:
        copy.wait()


def on_device(partials, scales, overflow_pos, weights, exponent):
    inter_size = lax.axis_size("inter")
    intra_size = lax.axis_size("intra")
    total = inter_size * intra_size
    row_total, full_width = partials.shape[1], partials.shape[2]
    block_total = scales.shape[2]
    block_len = full_width // block_total
    share_cols = full_width // intra_size
    blocks = share_cols // block_len
    width = share_cols // 2 + LANES
    any_space = pl.BlockSpec(memory_space=pl.ANY)
    vmem = pl.BlockSpec(memory_space=pltpu.VMEM)
    smem = pl.BlockSpec(memory_space=pltpu.SMEM)
    results = pl.pallas_call(
        functools.partial(exchange, inter_size, intra_size, block_len),
        out_shape=(
            pltpu.VMEM((1, share_cols), jnp.float32),
            pltpu.VMEM((1, blocks), jnp.float32),
            pltpu.VMEM((1, share_cols), jnp.float32),
            pltpu.VMEM((1, 2 * LANES), jnp.int32),
        ),
        in_specs=[any_space] * 5,
        out_specs=(vmem, vmem, vmem, vmem),
        scratch_shapes=[
            pltpu.VMEM((row_total, full_width), jnp.bfloat16),
            pltpu.VMEM((row_total, block_total), jnp.bfloat16),
            pltpu.SMEM((1, 1), jnp.int32),
            pltpu.VMEM((1, share_cols), jnp.float32),
            pltpu.SMEM((1,), jnp.int32),
            pltpu.VMEM((ROW_GROUP, intra_size, 2, width), jnp.float32),
            pltpu.VMEM((row_total, intra_size, 2, width), jnp.bfloat16),
            pltpu.VMEM((total, 2, width), jnp.bfloat16),
            pltpu.SemaphoreType.DMA((5,)),
            pltpu.SemaphoreType.DMA,
            pltpu.SemaphoreType.DMA,
            pltpu.SemaphoreType.DMA,
        ],
        compiler_params=pltpu.CompilerParams(collective_id=0, has_side_effects=True),
        name="exchange",
    )(partials, scales, overflow_pos, weights, exponent.reshape(1))
    grad_out, block_scale, master_out, new_exponent, count = pl.pallas_call(
        finish,
        out_shape=(
            jax.ShapeDtypeStruct((1, share_cols), jnp.float32),
            jax.ShapeDtypeStruct((1, blocks), jnp.float32),
            jax.ShapeDtypeStruct((1, share_cols), jnp.float32),
            jax.ShapeDtypeStruct((1,), jnp.int32),
            jax.ShapeDtypeStruct((1,), jnp.int32),
        ),
        in_specs=[vmem] * 4,
        out_specs=(any_space, any_space, any_space, smem, smem),
        scratch_shapes=[pltpu.SemaphoreType.DMA((3,))],
        name="finish",
    )(*(pltpu.with_memory_space_constraint(result, pltpu.VMEM) for result in results))
    return grad_out, block_scale, master_out, new_exponent.reshape(()), count.reshape(())


def solution(mesh):
    placed = (
        P(("inter", "intra"), None, None),
        P(("inter", "intra"), None, None),
        P(("inter", "intra"), None),
        P("inter", "intra"),
        P(),
    )
    return jax.shard_map(
        on_device,
        mesh=mesh,
        in_specs=placed,
        out_specs=(P("inter", "intra"), P("inter", "intra"), P("inter", "intra"), P(), P()),
        check_vma=False,
    )
```

time: 15.5 us -> 14.7 us (0.948)
  Pallas kernels: 13.4 us -> 12.6 us
    pallas_call x1, Pallas kernels: 11.9 us -> 11.4 us  [on_device(): pl.pallas_call(functools.partial(exchange, inter_size, intra_size, block_...]
    pallas_call x1, Pallas kernels: 1.46 us -> 1.16 us  [on_device(): pl.pallas_call(finish, out_shape=(jax.ShapeDtypeStruct((1, share_cols), j...]
where the time goes in v2:
time: 14.7 us; the launch traced here: 14.5 us
  Pallas kernels  12.6 us (86%)
  between operations  1.93 us (13%)
    pallas_call x1, Pallas kernels, on_device(): pl.pallas_call(functools.partial(exchange, inter_size, intra_size, block_...  11.4 us
    pallas_call x1, Pallas kernels, on_device(): pl.pallas_call(finish, out_shape=(jax.ShapeDtypeStruct((1, share_cols), j...  1.16 us

profile of v2, /device:TPU:0, one launch (start us, length us, event | category | flops | bytes accessed | tf_op | source)
XLA Modules:
  0.0 14.5 jit_solution(2436798236350054645)
XLA Ops:
  1.9 11.4 %exchange.1 = (f32[1,2560]{1,0:T(1,128)S(1)}, f32[1,10]{1,0:T(1,128)S(1)}, f32[1,2560]{1,0:T(1,128)S(1)}, s32[1,256]{1,0:T(1,128)S(1)}) custom-call(bf16[1,16,5120]{2,1,0:T(8,128)(2,1)} %x_hbm.1, bf16[1,16,20]{2,1,0:T(8,128)(2,1)} %s_hbm.1, s32[1,1]{1,0:T(1,128)S(6)} %copy.10.pos_hbm, f32[1,2560]{1,0:T(1,128)} %w_hbm.1, s32[1]{0:T(128)} %bitcast.3.e_hbm), custom_call_target="tpu_custom_call" | custom-call | tf_op jit(solution)/shard_map/exchange/pallas_call | solution.py:181
  13.4 1.2 %finish.1 = (f32[1,2560]{1,0:T(1,128)}, f32[1,10]{1,0:T(1,128)}, f32[1,2560]{1,0:T(1,128)}, s32[1]{0:T(128)}, s32[1]{0:T(128)}) custom-call(f32[1,2560]{1,0:T(1,128)S(1)} %get-tuple-element.14.grad_in, f32[1,10]{1,0:T(1,128)S(1)} %get-tuple-element.15.scale_in, f32[1,2560]{1,0:T(1,128)S(1)} %get-tuple-element.16.master_in, ...), custom_call_target="tpu_custom_call" | custom-call | tf_op jit(solution)/shard_map/finish/pallas_call | solution.py:208

commit v3 on v2

--- a/solution.py
+++ b/solution.py
@@ -53,11 +53,12 @@
         else:
             lax.fori_loop(1, total, lambda k, carry: (visit(k), carry)[1], 0)
 
-    def greet(k):
-        pl.semaphore_signal(barrier, inc=1, device_id=peer(k), device_id_type=pl.DeviceIdType.MESH)
-
-    if True:
-        each_peer(greet)
+    def greet(target):
+        pl.semaphore_signal(barrier, inc=1, device_id=(target // intra_size, target % intra_size), device_id_type=pl.DeviceIdType.MESH)
+
+    if True:
+        for n in range(total):
+            greet(n)
 
     for load in loads[:3]:
         load.wait()
@@ -87,10 +88,10 @@
     own = pltpu.make_async_copy(outgoing.at[my_inter, my_intra], incoming.at[me], own_sem)
     own.start()
     if True:
-        pl.semaphore_wait(barrier, total - 1)
-
-    def send(k):
-        to_inter, to_intra = peer(k)
+        pl.semaphore_wait(barrier, total)
+
+    def send(target):
+        to_inter, to_intra = target // intra_size, target % intra_size
         pltpu.make_async_remote_copy(
             src_ref=outgoing.at[to_inter, to_intra],
             dst_ref=incoming.at[me],
@@ -101,7 +102,8 @@
         ).start()
 
     if True:
-        each_peer(send)
+        for n in range(total - 1):
+            send(n + (n >= me).astype(jnp.int32))
     for load in loads[3:]:
         load.wait()
     exponent = e_ref[0]

time: 14.7 us -> 14.2 us (0.966)
  Pallas kernels: 12.6 us -> 12.1 us
    pallas_call x1, Pallas kernels: 11.4 us -> 10.9 us  [on_device(): pl.pallas_call(functools.partial(exchange, inter_size, intra_size, block_...]
where the time goes in v3:
time: 14.2 us; the launch traced here: 14 us
  Pallas kernels  12.1 us (85%)
  between operations  1.93 us (14%)
    pallas_call x1, Pallas kernels, on_device(): pl.pallas_call(functools.partial(exchange, inter_size, intra_size, block_...  10.9 us
    pallas_call x1, Pallas kernels, on_device(): pl.pallas_call(finish, out_shape=(jax.ShapeDtypeStruct((1, share_cols), j...  1.16 us

profile of v3, /device:TPU:0, one launch (start us, length us, event | category | flops | bytes accessed | tf_op | source)
XLA Modules:
  0.0 14.0 jit_solution(4594579365459464275)
XLA Ops:
  1.9 10.9 %exchange.1 = (f32[1,2560]{1,0:T(1,128)S(1)}, f32[1,10]{1,0:T(1,128)S(1)}, f32[1,2560]{1,0:T(1,128)S(1)}, s32[1,256]{1,0:T(1,128)S(1)}) custom-call(bf16[1,16,5120]{2,1,0:T(8,128)(2,1)} %x_hbm.1, bf16[1,16,20]{2,1,0:T(8,128)(2,1)} %s_hbm.1, s32[1,1]{1,0:T(1,128)S(6)} %copy.10.pos_hbm, f32[1,2560]{1,0:T(1,128)} %w_hbm.1, s32[1]{0:T(128)} %bitcast.3.e_hbm), custom_call_target="tpu_custom_call" | custom-call | tf_op jit(solution)/shard_map/exchange/pallas_call | solution.py:183
  12.8 1.2 %finish.1 = (f32[1,2560]{1,0:T(1,128)}, f32[1,10]{1,0:T(1,128)}, f32[1,2560]{1,0:T(1,128)}, s32[1]{0:T(128)}, s32[1]{0:T(128)}) custom-call(f32[1,2560]{1,0:T(1,128)S(1)} %get-tuple-element.14.grad_in, f32[1,10]{1,0:T(1,128)S(1)} %get-tuple-element.15.scale_in, f32[1,2560]{1,0:T(1,128)S(1)} %get-tuple-element.16.master_in, ...), custom_call_target="tpu_custom_call" | custom-call | tf_op jit(solution)/shard_map/finish/pallas_call | solution.py:210
